TPU v7x, 32 devices: a whole 2x2x4 slice. The times are simulated.
32 devices in a mesh: rows: 8 (over z, y), grp: 4 (over x, core).
Axes of the slice: x: 2, y: 2, z: 4, core: 2. Of those that a mesh axis runs over, the one named last changes fastest.
Arguments:
- basis: float32 [32, 65536], P(None, ('rows', 'grp')), may hold values from -0.03125 to 0.03125, as said below
- core: float32 [32, 32], replicated, may hold values from -0.3 to 4
- snapshots: bfloat16 [4, 32, 65536], P(None, 'grp', 'rows'), may hold values from -16 to 16
Outputs:
- new_basis: float32 [32, 65536], P(None, ('rows', 'grp'))
- new_core: float32 [32, 32], replicated
- first_coeffs: float32 [4, 32, 32], replicated
Inputs may be any that keep to these rules, and one draw needn't show every extreme that they name: `basis`: rows orthonormal up to float32 rounding.
All inputs are finite; a program needn't handle non-finite values.
Results may differ from a plain program's by a relative error of at most 0.0003.
Values may be sent and summed in bfloat16 or wider, within the bound.
A program may use at most 64 MiB of HBM per device.

v0:
```python
import jax
import jax.numpy as jnp
from jax import lax
from jax.sharding import PartitionSpec as P

BATCHES = 4


epsilon = 1e-06


def contract_rows(left, right):
    return lax.dot_general(
        left,
        right,
        (((1,), (1,)), ((), ())),
        precision=lax.Precision.HIGHEST,
        preferred_element_type=jnp.float32,
    )


def matmul(left, right):
    return jnp.dot(left, right, precision=lax.Precision.HIGHEST, preferred_element_type=jnp.float32)


def lower_solve(factor, right):
    return lax.linalg.triangular_solve(factor, right, left_side=True, lower=True)


def small_update(core_now, total, lower):
    rank = core_now.shape[0]
    cols = lower.shape[0]
    top = jnp.concatenate([core_now, total], axis=1)
    bottom = jnp.concatenate([jnp.zeros((cols, rank), jnp.float32), lower.T], axis=1)
    stacked = jnp.concatenate([top, bottom], axis=0)
    moment = matmul(stacked, stacked.T)
    leading = moment[:, :rank]
    factor = jnp.linalg.cholesky(matmul(leading.T, leading))
    rotation = lower_solve(factor, leading.T).T
    fresh_core = jnp.linalg.cholesky(matmul(rotation.T, matmul(moment, rotation)))
    return (rotation, fresh_core)


def body(basis, core, snapshots):
    rank = basis.shape[0]
    basis_now = basis
    core_now = core
    firsts = []
    gram_basis = lax.psum(contract_rows(basis_now, basis_now), ("rows", "grp"))
    for batch in range(BATCHES):
        columns = lax.all_to_all(snapshots[batch], "grp", split_axis=1, concat_axis=0, tiled=True)
        raw = columns.astype(jnp.float32)
        raw_cross, raw_gram = lax.psum(
            (contract_rows(basis_now, raw), contract_rows(raw, raw)), ("rows", "grp")
        )
        inverse = lax.rsqrt(jnp.diagonal(raw_gram) + epsilon)
        scaled = raw * inverse[:, None]
        cross = raw_cross * inverse[None, :]
        gram_raw = raw_gram * inverse[:, None] * inverse[None, :]
        second = cross - matmul(gram_basis, cross)
        total = cross + second
        basis_cross = cross - matmul(gram_basis, total)
        gram = (
            gram_raw
            - matmul(total.T, cross)
            - matmul(cross.T, total)
            + matmul(total.T, matmul(gram_basis, total))
        )
        twice = scaled - matmul(total.T, basis_now)
        lower = jnp.linalg.cholesky(gram)
        fresh = lower_solve(lower, twice)
        rotation, core_now = small_update(core_now, total, lower)
        cross_fresh = lower_solve(lower, basis_cross.T).T
        halfway = lower_solve(lower, gram)
        gram_fresh = lower_solve(lower, halfway.T).T
        upper_block = jnp.concatenate([gram_basis, cross_fresh], axis=1)
        lower_block = jnp.concatenate([cross_fresh.T, gram_fresh], axis=1)
        combined = jnp.concatenate([upper_block, lower_block], axis=0)
        gram_basis = matmul(rotation.T, matmul(combined, rotation))
        firsts.append(cross)
        basis_now = matmul(rotation[:rank].T, basis_now) + matmul(rotation[rank:].T, fresh)
    return (basis_now, core_now, jnp.stack(firsts, axis=0))


def solution(mesh):
    return jax.shard_map(
        body,
        mesh=mesh,
        in_specs=(P(None, ("rows", "grp")), P(), P(None, "grp", "rows")),
        out_specs=(P(None, ("rows", "grp")), P(), P()),
        check_vma=False,
    )
```

profile of v0, /device:TPU:0, one launch (start us, length us, event | category | flops | bytes accessed | tf_op | source)
XLA Modules:
  0.0 283.6 jit_solution(1562950860485663812)
XLA Ops:
  2.6 4.4 %all-to-all-start = ((bf16[8,4,2048]{2,0,1:T(8,128)(2,1)}), bf16[8,4,2048]{2,0,1:T(8,128)(2,1)S(1)}, u32[]{:S(2)}, u32[]{:S(2)}) async-start(bf16[8,4,2048]{2,0,1:T(8,128)(2,1)} %bitcast), calls=%async_computation | async-start | bytes 262144 | tf_op jit(solution)/shard_map/all_to_all | solution.py:51
  7.4 4.1 %all-to-all-done = bf16[8,4,2048]{2,0,1:T(8,128)(2,1)S(1)} async-done(((bf16[8,4,2048]{2,0,1:T(8,128)(2,1)}), bf16[8,4,2048]{2,0,1:T(8,128)(2,1)S(1)}, u32[]{:S(2)}, u32[]{:S(2)}) %all-to-all-start) | async-done | bytes 131104 | tf_op jit(solution)/shard_map/all_to_all | solution.py:51
  11.6 3.3 %all-to-all-start.1 = ((bf16[8,4,2048]{2,0,1:T(8,128)(2,1)}), bf16[8,4,2048]{2,0,1:T(8,128)(2,1)S(1)}, u32[]{:S(2)}, u32[]{:S(2)}) async-start(bf16[8,4,2048]{2,0,1:T(8,128)(2,1)} %bitcast.15), calls=%async_computation.1 | async-start | bytes 262144 | tf_op jit(solution)/shard_map/all_to_all | solution.py:51
  15.3 42.1 %all-reduce.7 = (f32[32,32]{1,0:T(8,128)S(1)}, f32[32,32]{0,1:T(8,128)S(1)}, f32[32,32]{0,1:T(8,128)S(1)}) all-reduce(f32[32,32]{1,0:T(8,128)S(1)} %fusion.230, f32[32,32]{0,1:T(8,128)S(1)} %fusion.18, f32[32,32]{0,1:T(8,128)S(1)} %fusion.16), channel_id=1, replica_groups=mesh['rows'=8,'grp'=4] {'rows','grp'}, use_global_device_ids=true, to_apply=%region_2.0 | all-reduce | flops 3072 | bytes 24576 | tf_op jit(solution)/shard_map/psum | solution.py:49
  59.3 2.9 %cholesky.194 = f32[32,32]{1,0:T(8,128)S(1)} custom-call(f32[32,32]{1,0:T(8,128)S(1)} %fusion.134), custom_call_target="Cholesky" | custom-call | tf_op jit(solution)/shard_map/jit(cholesky)/cholesky | solution.py:70
  63.6 2.4 custom-call.34
  67.2 2.9 %cholesky.205 = f32[32,32]{1,0:T(8,128)S(1)} custom-call(f32[32,32]{1,0:T(8,128)S(1)} %fusion.133), custom_call_target="Cholesky" | custom-call | tf_op jit(solution)/shard_map/jit(cholesky)/cholesky | solution.py:38
  71.4 2.4 custom-call.33
  76.5 3.5 %all-to-all-start.2 = ((bf16[8,4,2048]{2,0,1:T(8,128)(2,1)}), bf16[8,4,2048]{2,0,1:T(8,128)(2,1)S(1)}, u32[]{:S(2)}, u32[]{:S(2)}) async-start(bf16[8,4,2048]{2,0,1:T(8,128)(2,1)} %bitcast.39), calls=%async_computation.2 | async-start | bytes 262144 | tf_op jit(solution)/shard_map/all_to_all | solution.py:51
  80.4 41.5 %all-reduce.6 = (f32[32,32]{0,1:T(8,128)S(1)}, f32[32,32]{0,1:T(8,128)S(1)}) all-reduce(f32[32,32]{0,1:T(8,128)S(1)} %fusion.14, f32[32,32]{0,1:T(8,128)S(1)} %fusion.12), channel_id=1, replica_groups=mesh['rows'=8,'grp'=4] {'rows','grp'}, use_global_device_ids=true, to_apply=%region_5.9 | all-reduce | flops 2048 | bytes 16384 | tf_op jit(solution)/shard_map/psum | solution.py:53
  123.5 2.9 %cholesky.216 = f32[32,32]{1,0:T(8,128)S(1)} custom-call(f32[32,32]{1,0:T(8,128)S(1)} %fusion.129), custom_call_target="Cholesky" | custom-call | tf_op jit(solution)/shard_map/jit(cholesky)/cholesky | solution.py:40
  128.5 2.9 %cholesky.227 = f32[32,32]{1,0:T(8,128)S(1)} custom-call(f32[32,32]{1,0:T(8,128)S(1)} %fusion.121), custom_call_target="Cholesky" | custom-call | tf_op jit(solution)/shard_map/jit(cholesky)/cholesky | solution.py:70
  132.8 2.4 custom-call.39
  136.4 2.9 %cholesky.238 = f32[32,32]{1,0:T(8,128)S(1)} custom-call(f32[32,32]{1,0:T(8,128)S(1)} %fusion.120), custom_call_target="Cholesky" | custom-call | tf_op jit(solution)/shard_map/jit(cholesky)/cholesky | solution.py:38
  145.7 3.5 %all-to-all-start.3 = ((bf16[8,4,2048]{2,0,1:T(8,128)(2,1)}), bf16[8,4,2048]{2,0,1:T(8,128)(2,1)S(1)}, u32[]{:S(2)}, u32[]{:S(2)}) async-start(bf16[8,4,2048]{2,0,1:T(8,128)(2,1)} %bitcast.63), calls=%async_computation.3 | async-start | bytes 262144 | tf_op jit(solution)/shard_map/all_to_all | solution.py:51
  149.7 40.7 %all-reduce.5 = (f32[32,32]{0,1:T(8,128)S(1)}, f32[32,32]{0,1:T(8,128)S(1)}) all-reduce(f32[32,32]{0,1:T(8,128)S(1)} %fusion.10, f32[32,32]{0,1:T(8,128)S(1)} %fusion.8), channel_id=1, replica_groups=mesh['rows'=8,'grp'=4] {'rows','grp'}, use_global_device_ids=true, to_apply=%region_7.12 | all-reduce | flops 2048 | bytes 16384 | tf_op jit(solution)/shard_map/psum | solution.py:53
  192.0 2.9 %cholesky.249 = f32[32,32]{1,0:T(8,128)S(1)} custom-call(f32[32,32]{1,0:T(8,128)S(1)} %fusion.116), custom_call_target="Cholesky" | custom-call | tf_op jit(solution)/shard_map/jit(cholesky)/cholesky | solution.py:40
  197.0 2.9 %cholesky.260 = f32[32,32]{1,0:T(8,128)S(1)} custom-call(f32[32,32]{1,0:T(8,128)S(1)} %fusion.108), custom_call_target="Cholesky" | custom-call | tf_op jit(solution)/shard_map/jit(cholesky)/cholesky | solution.py:70
  204.8 2.9 %cholesky.271 = f32[32,32]{1,0:T(8,128)S(1)} custom-call(f32[32,32]{1,0:T(8,128)S(1)} %fusion.107), custom_call_target="Cholesky" | custom-call | tf_op jit(solution)/shard_map/jit(cholesky)/cholesky | solution.py:38
  214.6 39.8 %all-reduce.4 = (f32[32,32]{0,1:T(8,128)S(1)}, f32[32,32]{0,1:T(8,128)S(1)}) all-reduce(f32[32,32]{0,1:T(8,128)S(1)} %fusion.6, f32[32,32]{0,1:T(8,128)S(1)} %fusion.4), channel_id=1, replica_groups=mesh['rows'=8,'grp'=4] {'rows','grp'}, use_global_device_ids=true, to_apply=%region_9.14 | all-reduce | flops 2048 | bytes 16384 | tf_op jit(solution)/shard_map/psum | solution.py:53
  256.1 2.9 %cholesky.282 = f32[32,32]{1,0:T(8,128)S(1)} custom-call(f32[32,32]{1,0:T(8,128)S(1)} %fusion.103), custom_call_target="Cholesky" | custom-call | tf_op jit(solution)/shard_map/jit(cholesky)/cholesky | solution.py:40
  261.8 2.9 %cholesky.293 = f32[32,32]{1,0:T(8,128)S(1)} custom-call(f32[32,32]{1,0:T(8,128)S(1)} %fusion.95), custom_call_target="Cholesky" | custom-call | tf_op jit(solution)/shard_map/jit(cholesky)/cholesky | solution.py:70
  269.0 2.9 %cholesky.304 = f32[32,32]{1,0:T(8,128)S(1)} custom-call(f32[32,32]{1,0:T(8,128)S(1)} %fusion.94), custom_call_target="Cholesky" | custom-call | tf_op jit(solution)/shard_map/jit(cholesky)/cholesky | solution.py:38
  276.5 2.9 %cholesky.315 = f32[32,32]{1,0:T(8,128)S(1)} custom-call(f32[32,32]{1,0:T(8,128)S(1)} %fusion.88), custom_call_target="Cholesky" | custom-call | tf_op jit(solution)/shard_map/jit(cholesky)/cholesky | solution.py:40
  (178 shorter events, 56.8 us)
Async XLA Ops:
  0.6 6.4 %copy-start = (f32[32,2048]{1,0:T(8,128)S(1)}, f32[32,2048]{1,0:T(8,128)}, u32[]{:S(2)}) copy-start(f32[32,2048]{1,0:T(8,128)} %param.10) | copy-start | bytes 786436
  2.6 4.4 %copy-start.1 = (f32[32,32]{1,0:T(8,128)S(1)}, f32[32,32]{1,0:T(8,128)}, u32[]{:S(2)}) copy-start(f32[32,32]{1,0:T(8,128)} %param.11) | copy-start | bytes 12292
  2.6 9.0 %all-to-all-start = ((bf16[8,4,2048]{2,0,1:T(8,128)(2,1)}), bf16[8,4,2048]{2,0,1:T(8,128)(2,1)S(1)}, u32[]{:S(2)}, u32[]{:S(2)}) async-start(bf16[8,4,2048]{2,0,1:T(8,128)(2,1)} %bitcast), calls=%async_computation | async-start | bytes 262144 | tf_op jit(solution)/shard_map/all_to_all | solution.py:51
  11.6 64.9 %all-to-all-start.1 = ((bf16[8,4,2048]{2,0,1:T(8,128)(2,1)}), bf16[8,4,2048]{2,0,1:T(8,128)(2,1)S(1)}, u32[]{:S(2)}, u32[]{:S(2)}) async-start(bf16[8,4,2048]{2,0,1:T(8,128)(2,1)} %bitcast.15), calls=%async_computation.1 | async-start | bytes 262144 | tf_op jit(solution)/shard_map/all_to_all | solution.py:51
  76.5 69.2 %all-to-all-start.2 = ((bf16[8,4,2048]{2,0,1:T(8,128)(2,1)}), bf16[8,4,2048]{2,0,1:T(8,128)(2,1)S(1)}, u32[]{:S(2)}, u32[]{:S(2)}) async-start(bf16[8,4,2048]{2,0,1:T(8,128)(2,1)} %bitcast.39), calls=%async_computation.2 | async-start | bytes 262144 | tf_op jit(solution)/shard_map/all_to_all | solution.py:51
  145.7 68.5 %all-to-all-start.3 = ((bf16[8,4,2048]{2,0,1:T(8,128)(2,1)}), bf16[8,4,2048]{2,0,1:T(8,128)(2,1)S(1)}, u32[]{:S(2)}, u32[]{:S(2)}) async-start(bf16[8,4,2048]{2,0,1:T(8,128)(2,1)} %bitcast.63), calls=%async_computation.3 | async-start | bytes 262144 | tf_op jit(solution)/shard_map/all_to_all | solution.py:51
where the time goes:
time: 285 us; the launch traced here: 284 us
  blocking collectives  164 us (58%)
  other arithmetic  71.8 us (25%)
  matrix products  20.3 us (7%)
  starting transfers between devices  14.7 us (5%)
  local copies, waits for them, and re-layouts  7.12 us (2%)
  waiting for transfers between devices  4.15 us (1%)
    psum x3, blocking collectives, body(): lax.psum((contract_rows(basis_now, raw), contract_rows(raw, raw)), ('rows...  122 us
    psum x1, blocking collectives, body(): gram_basis = lax.psum(contract_rows(basis_now, basis_now), ('rows', 'grp'))  42.1 us
    another operation x16, other arithmetic, lower_solve(): lax.linalg.triangular_solve(factor, right, left_side=True, lower=True)  24.7 us
    all_to_all x4, starting transfers between devices, body(): lax.all_to_all(snapshots[batch], 'grp', split_axis=1, concat_axis=0, tile...  14.7 us
    another operation x12, other arithmetic, small_update(): jnp.linalg.cholesky(matmul(rotation.T, matmul(moment, rotation)))  14.7 us
    another operation x12, other arithmetic, small_update(): factor = jnp.linalg.cholesky(matmul(leading.T, leading))  14.4 us
    another operation x12, other arithmetic, body(): lower = jnp.linalg.cholesky(gram)  14.4 us
    dot_general x54, matrix products, matmul(): jnp.dot(left, right, precision=lax.Precision.HIGHEST, preferred_element_t...  13.7 us
  transfers between devices with their start and end apart: 4, of which 1 were waited for; matrix products, arithmetic and copies ran while one was open for 24% of the time, Pallas kernels for 0%

commit v1 on v0

v1 whole, which is shorter than its diff:
```python
import functools

import jax
import jax.numpy as jnp
from jax import lax
from jax.experimental import pallas as pl
from jax.experimental.pallas import tpu as pltpu
from jax.sharding import PartitionSpec as P

epsilon = 1e-06
BLOCK_ROWS = 8
MESH = pl.DeviceIdType.MESH


def mm(left, right):
    return lax.dot_general(
        left, right, (((1,), (0,)), ((), ())), precision=lax.Precision.HIGHEST, preferred_element_type=jnp.float32
    )


def mt(left, right):
    return lax.dot_general(
        left, right, (((1,), (1,)), ((), ())), precision=lax.Precision.HIGHEST, preferred_element_type=jnp.float32
    )


def split(x):
    high = x.astype(jnp.bfloat16)
    rest = x - high.astype(jnp.float32)
    mid = rest.astype(jnp.bfloat16)
    low = (rest - mid.astype(jnp.float32)).astype(jnp.bfloat16)
    return high, mid, low


def gram_kernel(
    nrows, ngrp, basis_ref, snap_ref, z_ref, sum_ref,
    raw, basis_v, z, part, landed, crossed, total,
    basis_sem, own_sem, z_sem, a2a_send, a2a_recv, rs_send, rs_recv, x_send, x_recv, ag_send, ag_recv,
):
    row, grp = lax.axis_index("rows"), lax.axis_index("grp")
    rank, width = basis_ref.shape
    members = BLOCK_ROWS * ngrp
    blocks = nrows // BLOCK_ROWS
    block = row // BLOCK_ROWS
    me = (row % BLOCK_ROWS) * ngrp + grp

    def device(q):
        return (block * BLOCK_ROWS + q // ngrp, q % ngrp)

    def peer(step):
        return lax.rem(me + step, members)

    def other(step):
        return (lax.rem(block + step, blocks) * BLOCK_ROWS + row % BLOCK_ROWS, grp)

    def piece(g):
        return snap_ref.at[:, :, pl.ds(pl.multiple_of(g * width, 128), width)]

    load_basis = pltpu.make_async_copy(basis_ref, basis_v, basis_sem)
    load_basis.start()
    load_own = pltpu.make_async_copy(piece(grp), raw.at[:, grp], own_sem)
    load_own.start()

    barrier = pltpu.get_barrier_semaphore()

    @pl.loop(1, members)
    def _(step):
        pl.semaphore_signal(barrier, inc=1, device_id=device(peer(step)), device_id_type=MESH)

    if blocks > 1:

        @pl.loop(1, blocks)
        def _(step):
            pl.semaphore_signal(barrier, inc=1, device_id=other(step), device_id_type=MESH)

    pl.semaphore_wait(barrier, members - 1 + blocks - 1)

    sends = []
    for step in range(1, ngrp):
        target = lax.rem(grp + step, ngrp)
        copy = pltpu.make_async_remote_copy(
            src_ref=piece(target), dst_ref=raw.at[:, grp],
            send_sem=a2a_send.at[step - 1], recv_sem=a2a_recv.at[step - 1],
            device_id=(row, target), device_id_type=MESH,
        )
        copy.start()
        sends.append(copy)

    load_basis.wait()
    high, mid, low = split(basis_v[...])
    columns = raw.shape[0] * raw.shape[1] * raw.shape[2]
    z[columns:columns + rank, :] = high
    z[columns + rank:columns + 2 * rank, :] = mid
    z[columns + 2 * rank:, :] = low
    load_own.wait()
    for copy in sends:
        copy.wait()
    z[:columns, :] = raw[...].astype(jnp.float32).reshape(columns, width).astype(jnp.bfloat16)
    store_z = pltpu.make_async_copy(z, z_ref, z_sem)
    store_z.start()
    zz = z[...]
    full = lax.dot_general(zz, zz, (((1,), (1,)), ((), ())), preferred_element_type=jnp.float32)
    basis_rows = full[columns:columns + rank] + full[columns + rank:columns + 2 * rank] + full[columns + 2 * rank:]
    cross = basis_rows[:, :columns]
    tail = jnp.concatenate([basis_rows[:, columns:], jnp.zeros((rank, columns - 3 * rank), jnp.float32)], axis=1)
    inner = tail + pltpu.roll(tail, columns - rank, 1) + pltpu.roll(tail, columns - 2 * rank, 1)
    lane = lax.broadcasted_iota(jnp.int32, (rank, columns), 1)
    first = full[:rank, :columns]
    second = jnp.where(lane < rank, inner, full[rank:2 * rank, :columns])
    last = pltpu.roll(full[3 * rank:4 * rank, :columns], rank, 1)
    third = jnp.where(lane < rank, last, full[2 * rank:3 * rank, :columns])
    size = part.shape[1]
    for i, value in enumerate((cross, first, second, third)):
        for j in range(rank // size):
            part[i * (rank // size) + j] = value[j * size:(j + 1) * size]

    @pl.loop(1, members)
    def _(step):
        target = peer(step)
        pltpu.make_async_remote_copy(
            src_ref=part.at[target], dst_ref=landed.at[step - 1],
            send_sem=rs_send, recv_sem=rs_recv, device_id=device(target), device_id_type=MESH,
        ).start()

    pltpu.make_async_copy(landed, landed, rs_recv).wait()
    mine = part[me] + jnp.sum(landed[...], axis=0)
    if blocks > 1:
        crossed[0] = mine

        @pl.loop(1, blocks)
        def _(step):
            pltpu.make_async_remote_copy(
                src_ref=crossed.at[0], dst_ref=crossed.at[step],
                send_sem=x_send, recv_sem=x_recv, device_id=other(step), device_id_type=MESH,
            ).start()

        rest = crossed.at[pl.ds(1, blocks - 1)]
        pltpu.make_async_copy(rest, rest, x_recv).wait()
        mine = jnp.sum(crossed[...], axis=0)
    total[me] = mine

    @pl.loop(1, members)
    def _(step):
        pltpu.make_async_remote_copy(
            src_ref=total.at[me], dst_ref=total.at[me],
            send_sem=ag_send, recv_sem=ag_recv, device_id=device(peer(step)), device_id_type=MESH,
        ).start()

    most = total.at[pl.ds(0, members - 1)]
    pltpu.make_async_copy(most, most, ag_recv).wait()
    for j in range(members):
        sum_ref[j * size:(j + 1) * size, :] = total[j]
    pltpu.make_async_copy(landed, landed, rs_send).wait()
    if blocks > 1:
        pltpu.make_async_copy(rest, rest, x_send).wait()
    pltpu.make_async_copy(most, most, ag_send).wait()
    store_z.wait()


def eliminate(matrix):
    n = matrix.shape[0]
    r = lax.broadcasted_iota(jnp.int32, (n, 1), 0)
    c = lax.broadcasted_iota(jnp.int32, (n, n), 1)
    eye = (c == lax.broadcasted_iota(jnp.int32, (n, n), 0)).astype(jnp.float32)
    work = jnp.concatenate([matrix, eye], axis=1)
    for k in range(n):
        row = work[k:k + 1, :]
        pivot = work[k:k + 1, k:k + 1]
        column = work[:, k:k + 1]
        factor = jnp.where(r > k, column / pivot, 0.0)
        work = jnp.where(r == k, work * lax.rsqrt(pivot), work - factor * row)
    return work[:, :n], work[:, n:]


def update_kernel(batches, sum_ref, core_ref, z_ref, basis_out, core_out, first_out, z, z_sem):
    load = pltpu.make_async_copy(z_ref, z, z_sem)
    load.start()
    rank = core_ref.shape[0]
    width = sum_ref.shape[1]
    lane = lax.broadcasted_iota(jnp.int32, (rank, width), 1)
    sub = lax.broadcasted_iota(jnp.int32, (rank, width), 0)
    kept = [sum_ref[rank * (1 + b):rank * (2 + b), :] for b in range(batches - 1)]
    kept.append(pltpu.roll(kept[-1], width - rank, 1))
    picks = [jnp.where(lane == sub + rank * b, kept[b], 0.0) for b in range(batches)]
    inverse_row = lax.rsqrt(jnp.sum(sum(picks), axis=0, keepdims=True) + epsilon)
    inverse_cols = [lax.rsqrt(jnp.sum(p, axis=1, keepdims=True) + epsilon) for p in picks]
    grams = [kept[b] * inverse_cols[b] * inverse_row for b in range(batches)]
    gram_basis = sum_ref[2 * rank:3 * rank, :rank]
    hits = sum_ref[:rank, :] * inverse_row
    coef_basis = (lane[:, :rank] == sub[:, :rank]).astype(jnp.float32)
    coef_raw = jnp.zeros((rank, width), jnp.float32)
    core = core_ref[...]
    energy = mt(core, core)
    for b in range(batches):
        cross = hits[:, b * rank:(b + 1) * rank]
        first_out[b] = cross
        total = cross + (cross - mm(gram_basis, cross))
        w1 = mm(energy, gram_basis) + mt(total, cross)
        w2 = mm(energy, cross) + mm(total, grams[b][:, b * rank:(b + 1) * rank])
        square = mt(w1, energy) + mt(w2, total)
        placed = [total]
        if b > 0:
            placed.insert(0, jnp.zeros((rank, b * rank), jnp.float32))
        if b < batches - 1:
            placed.append(jnp.zeros((rank, width - (b + 1) * rank), jnp.float32))
        v_basis = mm(energy, coef_basis)
        v_raw = mm(energy, coef_raw) + jnp.concatenate(placed, axis=1)
        v_hits = mm(energy, hits) + mm(total, grams[b])
        _, inverse = eliminate(square)
        coef_basis = mm(inverse, v_basis)
        coef_raw = mm(inverse, v_raw)
        hits = mm(inverse, v_hits)
        n1 = mm(inverse, w1)
        n2 = mm(inverse, w2)
        gram_basis = mt(mm(inverse, square), inverse)
        energy = mt(mm(n1, energy), n1) + mt(n2, n2)
    upper, _ = eliminate(energy)
    keep = lax.broadcasted_iota(jnp.int32, (rank, rank), 0) <= lax.broadcasted_iota(jnp.int32, (rank, rank), 1)
    core_out[...] = jnp.where(keep, upper, 0.0).T
    coef = jnp.concatenate([coef_raw * inverse_row] + [coef_basis] * 3, axis=1)
    pieces = jnp.concatenate([p.astype(jnp.float32) for p in split(coef)], axis=0).astype(jnp.bfloat16)
    load.wait()
    wide = jnp.dot(pieces, z[...], preferred_element_type=jnp.float32)
    basis_out[...] = wide[:rank] + wide[rank:2 * rank] + wide[2 * rank:]


def solution(mesh):
    nrows, ngrp = mesh.shape["rows"], mesh.shape["grp"]

    def body(basis, core, snapshots):
        rank, width = basis.shape
        batches, cols, _ = snapshots.shape
        columns = batches * cols * ngrp
        height = columns + 3 * rank
        members = BLOCK_ROWS * ngrp
        blocks = nrows // BLOCK_ROWS
        size = batches * rank // members
        vmem = pl.BlockSpec(memory_space=pltpu.VMEM)
        hbm = pl.BlockSpec(memory_space=pl.ANY)
        dma = pltpu.SemaphoreType.DMA
        z, sums = pl.pallas_call(
            functools.partial(gram_kernel, nrows, ngrp),
            out_shape=(
                jax.ShapeDtypeStruct((height, width), jnp.bfloat16),
                jax.ShapeDtypeStruct((batches * rank, columns), jnp.float32),
            ),
            in_specs=[hbm, hbm],
            out_specs=(hbm, vmem),
            scratch_shapes=[
                pltpu.VMEM((batches, ngrp, cols, width), jnp.bfloat16),
                pltpu.VMEM((rank, width), jnp.float32),
                pltpu.VMEM((height, width), jnp.bfloat16),
                pltpu.VMEM((members, size, columns), jnp.float32),
                pltpu.VMEM((members - 1, size, columns), jnp.float32),
                pltpu.VMEM((blocks, size, columns), jnp.float32),
                pltpu.VMEM((members, size, columns), jnp.float32),
                dma, dma, dma, dma((ngrp - 1,)), dma((ngrp - 1,)),
                dma, dma, dma, dma, dma, dma,
            ],
            compiler_params=pltpu.CompilerParams(collective_id=0, has_side_effects=True),
        )(basis, snapshots)
        return pl.pallas_call(
            functools.partial(update_kernel, batches),
            out_shape=(
                jax.ShapeDtypeStruct((rank, width), jnp.float32),
                jax.ShapeDtypeStruct((rank, rank), jnp.float32),
                jax.ShapeDtypeStruct((batches, rank, rank), jnp.float32),
            ),
            in_specs=[vmem, vmem, hbm],
            out_specs=(vmem, vmem, vmem),
            scratch_shapes=[pltpu.VMEM((height, width), jnp.bfloat16), dma],
        )(sums, core, z)

    return jax.shard_map(
        body,
        mesh=mesh,
        in_specs=(P(None, ("rows", "grp")), P(), P(None, "grp", "rows")),
        out_specs=(P(None, ("rows", "grp")), P(), P()),
        check_vma=False,
    )
```

time: 285 us -> 51.2 us (0.18)
  blocking collectives: 164 us -> 0 us
  other arithmetic: 71.8 us -> 0 us
  Pallas kernels: 0 us -> 50.3 us
  matrix products: 20.3 us -> 0 us
  starting transfers between devices: 14.7 us -> 0 us
  local copies, waits for them, and re-layouts: 7.12 us -> 0 us
  waiting for transfers between devices: 4.15 us -> 0 us
    psum x4 -> x0, blocking collectives: 164 us -> none  [the longest x3 122 us: body(): lax.psum((contract_rows(basis_now, raw), contract_rows(raw, raw)), ('rows...]
    another operation x57 -> x0, other arithmetic: 68.5 us -> none  [the longest x16 24.7 us: lower_solve(): lax.linalg.triangular_solve(factor, right, left_side=True, lower=True)]
    pallas_call x0 -> x2, Pallas kernels: none -> 50.3 us  [the longest x1 25.7 us: body(): pl.pallas_call(functools.partial(update_kernel, batches), out_shape=(jax....]
    dot_general x63 -> x0, matrix products: 15.8 us -> none  [the longest x54 13.7 us: matmul(): jnp.dot(left, right, precision=lax.Precision.HIGHEST, preferred_element_t...]
    all_to_all x4 -> x0, starting transfers between devices: 14.7 us -> none  [body(): lax.all_to_all(snapshots[batch], 'grp', split_axis=1, concat_axis=0, tile...]
    another operation x17 -> x0, matrix products: 4.42 us -> none  [lower_solve(): lax.linalg.triangular_solve(factor, right, left_side=True, lower=True)]
    all_to_all x4 -> x0, waiting for transfers between devices: 4.15 us -> none  [body(): lax.all_to_all(snapshots[batch], 'grp', split_axis=1, concat_axis=0, tile...]
    select_n x4 -> x0, other arithmetic: 3.2 us -> none  [small_update(): jnp.linalg.cholesky(matmul(rotation.T, matmul(moment, rotation)))]
  transfers between devices with their start and end apart: 4 -> 0, of which waited for: 1 -> 0; matrix products, arithmetic and copies ran while one was open for 24% -> 0% of each run, Pallas kernels for 0% -> 0%
where the time goes in v1:
time: 51.2 us; the launch traced here: 51 us
  Pallas kernels  50.3 us (98%)
  between operations  0.64 us (1%)
    pallas_call x1, Pallas kernels, body(): pl.pallas_call(functools.partial(update_kernel, batches), out_shape=(jax....  25.7 us
    pallas_call x1, Pallas kernels, body(): pl.pallas_call(functools.partial(gram_kernel, nrows, ngrp), out_shape=(ja...  24.7 us

profile of v1, /device:TPU:0, one launch (start us, length us, event | category | flops | bytes accessed | tf_op | source)
XLA Modules:
  0.0 51.0 jit_solution(17534139455859217175)
XLA Ops:
  0.6 24.7 %shard_map.58 = (bf16[224,2048]{1,0:T(8,128)(2,1)}, f32[128,128]{1,0:T(8,128)}) custom-call(f32[32,2048]{1,0:T(8,128)} %basis_ref.1, bf16[4,8,8192]{2,1,0:T(8,128)(2,1)} %snap_ref.1), custom_call_target="tpu_custom_call" | custom-call | tf_op jit(solution)/shard_map/pallas_call | solution.py:241
  25.3 25.7 %shard_map.59 = (f32[32,2048]{1,0:T(8,128)}, f32[32,32]{1,0:T(8,128)}, f32[4,32,32]{2,1,0:T(8,128)}) custom-call(f32[128,128]{1,0:T(8,128)} %get-tuple-element.5.sum_ref, f32[32,32]{1,0:T(8,128)} %core_ref.1, bf16[224,2048]{1,0:T(8,128)(2,1)} %get-tuple-element.6.z_ref), custom_call_target="tpu_custom_call" | custom-call | tf_op jit(solution)/shard_map/pallas_call | solution.py:262

commit v2 on v1

--- a/solution.py
+++ b/solution.py
@@ -157,19 +157,51 @@
     store_z.wait()
 
 
-def eliminate(matrix):
+def eliminate(matrix, want_lower=False):
     n = matrix.shape[0]
-    r = lax.broadcasted_iota(jnp.int32, (n, 1), 0)
-    c = lax.broadcasted_iota(jnp.int32, (n, n), 1)
-    eye = (c == lax.broadcasted_iota(jnp.int32, (n, n), 0)).astype(jnp.float32)
-    work = jnp.concatenate([matrix, eye], axis=1)
-    for k in range(n):
-        row = work[k:k + 1, :]
-        pivot = work[k:k + 1, k:k + 1]
-        column = work[:, k:k + 1]
-        factor = jnp.where(r > k, column / pivot, 0.0)
-        work = jnp.where(r == k, work * lax.rsqrt(pivot), work - factor * row)
-    return work[:, :n], work[:, n:]
+    tile = 8
+    tiles = n // tile
+    r = lax.broadcasted_iota(jnp.int32, (tile, n), 0)
+    c = lax.broadcasted_iota(jnp.int32, (tile, n), 1)
+    left = [matrix[t * tile:(t + 1) * tile] for t in range(tiles)]
+    if want_lower:
+        result = [jnp.zeros((tile, n), jnp.float32)] * tiles
+    else:
+        result = [(c == r + t * tile).astype(jnp.float32) for t in range(tiles)]
+    for t in range(tiles):
+        below = range(t, tiles)
+        panel = [
+            {u: jnp.broadcast_to(left[u][:, t * tile + j:t * tile + j + 1], (tile, n)) for u in below}
+            for j in range(tile)
+        ]
+        scale = jnp.ones((tile, n), jnp.float32)
+        for j in range(tile):
+            k = t * tile + j
+            column = panel[j]
+            pivot = column[t][j:j + 1]
+            inverse = 1.0 / pivot
+            root = lax.rsqrt(pivot)
+            if want_lower:
+                for u in below:
+                    keep = (c == k) & (r >= j) if u == t else c == k
+                    result[u] = jnp.where(keep, column[u] * root, result[u])
+            else:
+                scale = jnp.where(r == j, root, scale)
+            masked = {u: jnp.where(r > j, column[u], 0.0) if u == t else column[u] for u in below}
+            for l in range(j + 1, tile):
+                head = panel[l][t][j:j + 1]
+                for u in below:
+                    panel[l][u] = panel[l][u] - (masked[u] * head) * inverse
+            top = left[t][j:j + 1] * inverse
+            body = result[t][j:j + 1] * inverse
+            for u in below:
+                if t < tiles - 1:
+                    left[u] = left[u] - masked[u] * top
+                if not want_lower:
+                    result[u] = result[u] - masked[u] * body
+        if not want_lower:
+            result[t] = result[t] * scale
+    return jnp.concatenate(result, axis=0)
 
 
 def update_kernel(batches, sum_ref, core_ref, z_ref, basis_out, core_out, first_out, z, z_sem):
@@ -197,7 +229,8 @@
         total = cross + (cross - mm(gram_basis, cross))
         w1 = mm(energy, gram_basis) + mt(total, cross)
         w2 = mm(energy, cross) + mm(total, grams[b][:, b * rank:(b + 1) * rank])
-        square = mt(w1, energy) + mt(w2, total)
+        w1_energy = mm(w1, energy)
+        square = w1_energy + mt(w2, total)
         placed = [total]
         if b > 0:
             placed.insert(0, jnp.zeros((rank, b * rank), jnp.float32))
@@ -206,21 +239,19 @@
         v_basis = mm(energy, coef_basis)
         v_raw = mm(energy, coef_raw) + jnp.concatenate(placed, axis=1)
         v_hits = mm(energy, hits) + mm(total, grams[b])
-        _, inverse = eliminate(square)
+        inverse = eliminate(square)
         coef_basis = mm(inverse, v_basis)
         coef_raw = mm(inverse, v_raw)
         hits = mm(inverse, v_hits)
         n1 = mm(inverse, w1)
         n2 = mm(inverse, w2)
         gram_basis = mt(mm(inverse, square), inverse)
-        energy = mt(mm(n1, energy), n1) + mt(n2, n2)
-    upper, _ = eliminate(energy)
-    keep = lax.broadcasted_iota(jnp.int32, (rank, rank), 0) <= lax.broadcasted_iota(jnp.int32, (rank, rank), 1)
-    core_out[...] = jnp.where(keep, upper, 0.0).T
+        energy = mt(mm(inverse, w1_energy), n1) + mt(n2, n2)
     coef = jnp.concatenate([coef_raw * inverse_row] + [coef_basis] * 3, axis=1)
     pieces = jnp.concatenate([p.astype(jnp.float32) for p in split(coef)], axis=0).astype(jnp.bfloat16)
     load.wait()
     wide = jnp.dot(pieces, z[...], preferred_element_type=jnp.float32)
+    core_out[...] = eliminate(energy, want_lower=True)
     basis_out[...] = wide[:rank] + wide[rank:2 * rank] + wide[2 * rank:]
 
 

time: 51.2 us -> 36.6 us (0.71)
  Pallas kernels: 50.3 us -> 35.7 us
    pallas_call x1, Pallas kernels: 25.7 us -> 11 us  [body(): pl.pallas_call(functools.partial(update_kernel, batches), out_shape=(jax....]
where the time goes in v2:
time: 36.6 us; the launch traced here: 36.3 us
  Pallas kernels  35.7 us (98%)
  between operations  0.64 us (2%)
    pallas_call x1, Pallas kernels, body(): pl.pallas_call(functools.partial(gram_kernel, nrows, ngrp), out_shape=(ja...  24.7 us
    pallas_call x1, Pallas kernels, body(): pl.pallas_call(functools.partial(update_kernel, batches), out_shape=(jax....  11 us

profile of v2, /device:TPU:0, one launch (start us, length us, event | category | flops | bytes accessed | tf_op | source)
XLA Modules:
  0.0 36.3 jit_solution(1006172599705195799)
XLA Ops:
  0.6 24.7 %shard_map.58 = (bf16[224,2048]{1,0:T(8,128)(2,1)}, f32[128,128]{1,0:T(8,128)}) custom-call(f32[32,2048]{1,0:T(8,128)} %basis_ref.1, bf16[4,8,8192]{2,1,0:T(8,128)(2,1)} %snap_ref.1), custom_call_target="tpu_custom_call" | custom-call | tf_op jit(solution)/shard_map/pallas_call | solution.py:272
  25.3 11.0 %shard_map.59 = (f32[32,2048]{1,0:T(8,128)}, f32[32,32]{1,0:T(8,128)}, f32[4,32,32]{2,1,0:T(8,128)}) custom-call(f32[128,128]{1,0:T(8,128)} %get-tuple-element.5.sum_ref, f32[32,32]{1,0:T(8,128)} %core_ref.1, bf16[224,2048]{1,0:T(8,128)(2,1)} %get-tuple-element.6.z_ref), custom_call_target="tpu_custom_call" | custom-call | tf_op jit(solution)/shard_map/pallas_call | solution.py:293

commit v3 on v0

v3 whole, which is shorter than its diff:
```python
import functools

import jax
import jax.numpy as jnp
from jax import lax
from jax.experimental import pallas as pl
from jax.experimental.pallas import tpu as pltpu
from jax.sharding import PartitionSpec as P

epsilon = 1e-06
BLOCK_ROWS = 8
STAGES = ((0, 1), (1, 2), (2, 4))
GROUPS = (1, 1, 3)
MESH = pl.DeviceIdType.MESH


def mm(left, right):
    return lax.dot_general(
        left, right, (((1,), (0,)), ((), ())), precision=lax.Precision.HIGHEST, preferred_element_type=jnp.float32
    )


def mt(left, right):
    return lax.dot_general(
        left, right, (((1,), (1,)), ((), ())), precision=lax.Precision.HIGHEST, preferred_element_type=jnp.float32
    )


def split(x):
    high = x.astype(jnp.bfloat16)
    rest = x - high.astype(jnp.float32)
    mid = rest.astype(jnp.bfloat16)
    low = (rest - mid.astype(jnp.float32)).astype(jnp.bfloat16)
    return high, mid, low


def eliminate(matrix, want_lower=False):
    n = matrix.shape[0]
    tile = 8
    tiles = n // tile
    r = lax.broadcasted_iota(jnp.int32, (tile, n), 0)
    c = lax.broadcasted_iota(jnp.int32, (tile, n), 1)
    left = [matrix[t * tile:(t + 1) * tile] for t in range(tiles)]
    if want_lower:
        result = [jnp.zeros((tile, n), jnp.float32)] * tiles
    else:
        result = [(c == r + t * tile).astype(jnp.float32) for t in range(tiles)]
    for t in range(tiles):
        below = range(t, tiles)
        panel = [
            {u: jnp.broadcast_to(left[u][:, t * tile + j:t * tile + j + 1], (tile, n)) for u in below}
            for j in range(tile)
        ]
        scale = jnp.ones((tile, n), jnp.float32)
        for j in range(tile):
            k = t * tile + j
            column = panel[j]
            pivot = column[t][j:j + 1]
            inverse = 1.0 / pivot
            root = lax.rsqrt(pivot)
            if want_lower:
                for u in below:
                    keep = (c == k) & (r >= j) if u == t else c == k
                    result[u] = jnp.where(keep, column[u] * root, result[u])
            else:
                scale = jnp.where(r == j, root, scale)
            masked = {u: jnp.where(r > j, column[u], 0.0) if u == t else column[u] for u in below}
            for l in range(j + 1, tile):
                head = panel[l][t][j:j + 1]
                for u in below:
                    panel[l][u] = panel[l][u] - (masked[u] * head) * inverse
            top = left[t][j:j + 1] * inverse
            body = result[t][j:j + 1] * inverse
            for u in below:
                if t < tiles - 1:
                    left[u] = left[u] - masked[u] * top
                if not want_lower:
                    result[u] = result[u] - masked[u] * body
        if not want_lower:
            result[t] = result[t] * scale
    return jnp.concatenate(result, axis=0)


def fused_kernel(nrows, ngrp, basis_ref, core_ref, snap_ref, z_ref, coef_ref, energy_ref, first_ref, raw, basis_v, z, *scratch):
    count = len(STAGES)
    parts, landeds, crosseds, totals = (scratch[i * count:(i + 1) * count] for i in range(4))
    basis_sem, own_sem, z_sem, a2a_send, a2a_recv, rs_send, rs_recv, x_send, x_recv, ag_send, ag_recv = scratch[4 * count:]
    row, grp = lax.axis_index("rows"), lax.axis_index("grp")
    rank, width = basis_ref.shape
    batches, cols, _ = snap_ref.shape
    members = BLOCK_ROWS * ngrp
    blocks = nrows // BLOCK_ROWS
    block = row // BLOCK_ROWS
    me = (row % BLOCK_ROWS) * ngrp + grp

    def device(q):
        return (block * BLOCK_ROWS + q // ngrp, q % ngrp)

    def peer(step):
        return lax.rem(me + step, members)

    def other(step):
        return (lax.rem(block + step, blocks) * BLOCK_ROWS + row % BLOCK_ROWS, grp)

    def piece(g, start, stop):
        return snap_ref.at[start:stop, :, pl.ds(pl.multiple_of(g * width, 128), width)]

    load_basis = pltpu.make_async_copy(basis_ref, basis_v, basis_sem)
    load_basis.start()
    load_own = pltpu.make_async_copy(piece(grp, 0, batches), raw.at[:, grp], own_sem)
    load_own.start()

    barrier = pltpu.get_barrier_semaphore()

    @pl.loop(1, members)
    def _(step):
        pl.semaphore_signal(barrier, inc=1, device_id=device(peer(step)), device_id_type=MESH)

    if blocks > 1:

        @pl.loop(1, blocks)
        def _(step):
            pl.semaphore_signal(barrier, inc=1, device_id=other(step), device_id_type=MESH)

    pl.semaphore_wait(barrier, members - 1 + blocks - 1)

    sends = []
    for s, (start, stop) in enumerate(STAGES):
        stage = []
        for step in range(1, ngrp):
            target = lax.rem(grp + step, ngrp)
            copy = pltpu.make_async_remote_copy(
                src_ref=piece(target, start, stop), dst_ref=raw.at[start:stop, grp],
                send_sem=a2a_send.at[s, step - 1], recv_sem=a2a_recv.at[s, step - 1],
                device_id=(row, target), device_id_type=MESH,
            )
            copy.start()
            stage.append(copy)
        sends.append(stage)

    load_basis.wait()
    base = 3 * rank
    for i, value in enumerate(split(basis_v[...])):
        z[i * rank:(i + 1) * rank, :] = value
    load_own.wait()
    lane = lax.broadcasted_iota(jnp.int32, (rank, 4 * rank), 1)

    def products(left, right):
        return lax.dot_general(left, right, (((1,), (1,)), ((), ())), preferred_element_type=jnp.float32)

    def fold(x):
        return x + pltpu.roll(x, 3 * rank, 1) + pltpu.roll(x, 2 * rank, 1)

    def widen(x):
        missing = 4 * rank - x.shape[1]
        return x if missing == 0 else jnp.concatenate([x, jnp.zeros((rank, missing), jnp.float32)], axis=1)

    inner = products(z[:base, :], z[:base, :])
    inner = widen(inner[:rank] + inner[rank:2 * rank] + inner[2 * rank:])
    inner = pltpu.roll(fold(inner), rank, 1)

    def reduce_start(s):
        start, stop = STAGES[s]
        for copy in sends[s]:
            copy.wait()
        low, high = base + start * rank, base + stop * rank
        fresh = raw[start:stop].astype(jnp.float32).reshape(high - low, width).astype(jnp.bfloat16)
        z[low:high, :] = fresh
        full = products(fresh, z[:high, :])
        groups = []
        for b in range(start, stop):
            near = full[(b - start) * rank:(b - start + 1) * rank, :4 * rank]
            folded = jnp.where(lane < base, fold(jnp.where(lane < base, near, 0.0)), near)
            if b == 0:
                middle = inner
            else:
                far = widen(full[(b - start) * rank:(b - start + 1) * rank, 4 * rank:4 * rank + rank * b])
                middle = pltpu.roll(far, rank, 1)
            groups.append(jnp.where((lane >= rank) & (lane < base), middle, folded))
            if b == batches - 1:
                groups.append(far)
        packed = jnp.concatenate(groups, axis=0)
        size = parts[s].shape[1]
        for j in range(members):
            parts[s][j] = packed[j * size:(j + 1) * size]

        @pl.loop(1, members)
        def _(step):
            target = peer(step)
            pltpu.make_async_remote_copy(
                src_ref=parts[s].at[target], dst_ref=landeds[s].at[step - 1],
                send_sem=rs_send.at[s], recv_sem=rs_recv.at[s], device_id=device(target), device_id_type=MESH,
            ).start()

    def gather_start(s):
        landed, crossed, total = landeds[s], crosseds[s], totals[s]
        pltpu.make_async_copy(landed, landed, rs_recv.at[s]).wait()
        mine = parts[s][me] + jnp.sum(landed[...], axis=0)
        if blocks > 1:
            crossed[0] = mine

            @pl.loop(1, blocks)
            def _(step):
                pltpu.make_async_remote_copy(
                    src_ref=crossed.at[0], dst_ref=crossed.at[step],
                    send_sem=x_send.at[s], recv_sem=x_recv.at[s], device_id=other(step), device_id_type=MESH,
                ).start()

            rest = crossed.at[pl.ds(1, blocks - 1)]
            pltpu.make_async_copy(rest, rest, x_recv.at[s]).wait()
            mine = jnp.sum(crossed[...], axis=0)
        total[me] = mine

        @pl.loop(1, members)
        def _(step):
            pltpu.make_async_remote_copy(
                src_ref=total.at[me], dst_ref=total.at[me],
                send_sem=ag_send.at[s], recv_sem=ag_recv.at[s], device_id=device(peer(step)), device_id_type=MESH,
            ).start()

    def gather_wait(s):
        most = totals[s].at[pl.ds(0, members - 1)]
        pltpu.make_async_copy(most, most, ag_recv.at[s]).wait()
        size = parts[s].shape[1]
        values = jnp.concatenate([totals[s][j] for j in range(members)], axis=0)
        return [values[g * rank:(g + 1) * rank] for g in range(size)]

    sub = lax.broadcasted_iota(jnp.int32, (rank, rank), 0)
    eye = sub == lane[:, :rank]
    coef = (lane == lax.broadcasted_iota(jnp.int32, (rank, 4 * rank), 0)).astype(jnp.float32)
    core = core_ref[...]
    spots = (3, 1, 2)

    def update(b, state, cross_raw, own):
        coef, energy, gram_basis = state
        diagonal = jnp.where(eye, own, 0.0)
        inverse_col = lax.rsqrt(jnp.sum(diagonal, axis=1, keepdims=True) + epsilon)
        inverse_row = lax.rsqrt(jnp.sum(diagonal, axis=0, keepdims=True) + epsilon)
        cross = mt(coef, cross_raw * inverse_col)
        first_ref[b] = cross
        total = cross + (cross - mm(gram_basis, cross))
        w1 = mm(energy, gram_basis) + mt(total, cross)
        w2 = mm(energy, cross) + mm(total, own * inverse_col * inverse_row)
        w1_energy = mm(w1, energy)
        square = w1_energy + mt(w2, total)
        placed = total * inverse_row
        kept = mm(energy, coef)
        if b < batches - 1:
            at = spots[b]
            strip = widen(jnp.concatenate([jnp.zeros((rank, at * rank), jnp.float32), placed], axis=1))
            kept = kept + strip
        inverse = eliminate(square)
        coef = mm(inverse, kept)
        if b == batches - 1:
            coef = (coef, mm(inverse, placed))
        else:
            gram_basis = mt(mm(inverse, square), inverse)
        n1 = mm(inverse, w1)
        n2 = mm(inverse, w2)
        energy = mt(mm(inverse, w1_energy), n1) + mt(n2, n2)
        return coef, energy, gram_basis

    reduce_start(0)
    reduce_start(1)
    gather_start(0)
    reduce_start(2)
    store_z = pltpu.make_async_copy(z, z_ref, z_sem)
    store_z.start()
    gather_start(1)
    sums, = gather_wait(0)
    state = (coef, mt(core, core), sums[:, rank:2 * rank])
    gather_start(2)
    state = update(0, state, sums, sums[:, base:])
    sums, = gather_wait(1)
    state = update(1, state, sums, sums[:, rank:2 * rank])
    sums, later, last = gather_wait(2)
    state = update(2, state, sums, sums[:, 2 * rank:base])
    (coef, coef_last), energy, _ = update(3, state, later, last[:, 2 * rank:base])
    energy_ref[...] = energy
    blocks_of = [coef[:, i * rank:(i + 1) * rank] for i in range(4)]
    wide = jnp.concatenate([blocks_of[0]] * 3 + [blocks_of[3], blocks_of[1], blocks_of[2], coef_last], axis=1)
    coef_ref[...] = wide
    for s in range(count):
        pltpu.make_async_copy(landeds[s], landeds[s], rs_send.at[s]).wait()
        if blocks > 1:
            rest = crosseds[s].at[pl.ds(1, blocks - 1)]
            pltpu.make_async_copy(rest, rest, x_send.at[s]).wait()
        most = totals[s].at[pl.ds(0, members - 1)]
        pltpu.make_async_copy(most, most, ag_send.at[s]).wait()
    store_z.wait()


def final_kernel(coef_ref, energy_ref, first_ref, z_ref, basis_out, core_out, first_out, z, z_sem):
    load = pltpu.make_async_copy(z_ref, z, z_sem)
    load.start()
    rank = energy_ref.shape[0]
    first_out[...] = first_ref[...]
    pieces = jnp.concatenate([p.astype(jnp.float32) for p in split(coef_ref[...])], axis=0).astype(jnp.bfloat16)
    core_out[...] = eliminate(energy_ref[...], want_lower=True)
    load.wait()
    wide = jnp.dot(pieces, z[...], preferred_element_type=jnp.float32)
    basis_out[...] = wide[:rank] + wide[rank:2 * rank] + wide[2 * rank:]


def solution(mesh):
    nrows, ngrp = mesh.shape["rows"], mesh.shape["grp"]

    def body(basis, core, snapshots):
        rank, width = basis.shape
        batches, cols, _ = snapshots.shape
        height = batches * cols * ngrp + 3 * rank
        members = BLOCK_ROWS * ngrp
        blocks = nrows // BLOCK_ROWS
        count = len(STAGES)
        sizes = [groups * rank // members for groups in GROUPS]
        vmem = pl.BlockSpec(memory_space=pltpu.VMEM)
        hbm = pl.BlockSpec(memory_space=pl.ANY)
        dma = pltpu.SemaphoreType.DMA
        buffers = [
            pltpu.VMEM((slots, size, 4 * rank), jnp.float32)
            for slots in (members, members - 1, blocks, members)
            for size in sizes
        ]
        z, coef, energy, firsts = pl.pallas_call(
            functools.partial(fused_kernel, nrows, ngrp),
            out_shape=(
                jax.ShapeDtypeStruct((height, width), jnp.bfloat16),
                jax.ShapeDtypeStruct((rank, height), jnp.float32),
                jax.ShapeDtypeStruct((rank, rank), jnp.float32),
                jax.ShapeDtypeStruct((batches, rank, rank), jnp.float32),
            ),
            in_specs=[hbm, vmem, hbm],
            out_specs=(hbm, vmem, vmem, vmem),
            scratch_shapes=[
                pltpu.VMEM((batches, ngrp, cols, width), jnp.bfloat16),
                pltpu.VMEM((rank, width), jnp.float32),
                pltpu.VMEM((height, width), jnp.bfloat16),
                *buffers,
                dma, dma, dma, dma((count, ngrp - 1)), dma((count, ngrp - 1)),
                *[dma((count,))] * 6,
            ],
            compiler_params=pltpu.CompilerParams(collective_id=0, has_side_effects=True),
        )(basis, core, snapshots)
        return pl.pallas_call(
            final_kernel,
            out_shape=(
                jax.ShapeDtypeStruct((rank, width), jnp.float32),
                jax.ShapeDtypeStruct((rank, rank), jnp.float32),
                jax.ShapeDtypeStruct((batches, rank, rank), jnp.float32),
            ),
            in_specs=[vmem, vmem, vmem, hbm],
            out_specs=(vmem, vmem, vmem),
            scratch_shapes=[pltpu.VMEM((height, width), jnp.bfloat16), dma],
        )(coef, energy, firsts, z)

    return jax.shard_map(
        body,
        mesh=mesh,
        in_specs=(P(None, ("rows", "grp")), P(), P(None, "grp", "rows")),
        out_specs=(P(None, ("rows", "grp")), P(), P()),
        check_vma=False,
    )
```

time: 285 us -> 35.8 us (0.13)
  blocking collectives: 164 us -> 0 us
  other arithmetic: 71.8 us -> 0 us
  Pallas kernels: 0 us -> 34.9 us
  matrix products: 20.3 us -> 0 us
  starting transfers between devices: 14.7 us -> 0 us
  local copies, waits for them, and re-layouts: 7.12 us -> 0 us
  waiting for transfers between devices: 4.15 us -> 0 us
    psum x4 -> x0, blocking collectives: 164 us -> none  [the longest x3 122 us: body(): lax.psum((contract_rows(basis_now, raw), contract_rows(raw, raw)), ('rows...]
    another operation x57 -> x0, other arithmetic: 68.5 us -> none  [the longest x16 24.7 us: lower_solve(): lax.linalg.triangular_solve(factor, right, left_side=True, lower=True)]
    pallas_call x0 -> x2, Pallas kernels: none -> 34.9 us  [the longest x1 31.5 us: body(): pl.pallas_call(functools.partial(fused_kernel, nrows, ngrp), out_shape=(j...]
    dot_general x63 -> x0, matrix products: 15.8 us -> none  [the longest x54 13.7 us: matmul(): jnp.dot(left, right, precision=lax.Precision.HIGHEST, preferred_element_t...]
    all_to_all x4 -> x0, starting transfers between devices: 14.7 us -> none  [body(): lax.all_to_all(snapshots[batch], 'grp', split_axis=1, concat_axis=0, tile...]
    another operation x17 -> x0, matrix products: 4.42 us -> none  [lower_solve(): lax.linalg.triangular_solve(factor, right, left_side=True, lower=True)]
    all_to_all x4 -> x0, waiting for transfers between devices: 4.15 us -> none  [body(): lax.all_to_all(snapshots[batch], 'grp', split_axis=1, concat_axis=0, tile...]
    select_n x4 -> x0, other arithmetic: 3.2 us -> none  [small_update(): jnp.linalg.cholesky(matmul(rotation.T, matmul(moment, rotation)))]
  transfers between devices with their start and end apart: 4 -> 0, of which waited for: 1 -> 0; matrix products, arithmetic and copies ran while one was open for 24% -> 0% of each run, Pallas kernels for 0% -> 0%
where the time goes in v3:
time: 35.8 us; the launch traced here: 35.5 us
  Pallas kernels  34.9 us (97%)
  between operations  0.64 us (2%)
    pallas_call x1, Pallas kernels, body(): pl.pallas_call(functools.partial(fused_kernel, nrows, ngrp), out_shape=(j...  31.5 us
    pallas_call x1, Pallas kernels, body(): pl.pallas_call(final_kernel, out_shape=(jax.ShapeDtypeStruct((rank, width...  3.35 us

profile of v3, /device:TPU:0, one launch (start us, length us, event | category | flops | bytes accessed | tf_op | source)
XLA Modules:
  0.0 35.5 jit_solution(8350935555822837803)
XLA Ops:
  0.6 31.5 %shard_map.58 = (bf16[224,2048]{1,0:T(8,128)(2,1)}, f32[32,224]{1,0:T(8,128)}, f32[32,32]{1,0:T(8,128)}, f32[4,32,32]{2,1,0:T(8,128)}) custom-call(f32[32,2048]{1,0:T(8,128)} %basis_ref.1, f32[32,32]{1,0:T(8,128)} %core_ref.1, bf16[4,8,8192]{2,1,0:T(8,128)(2,1)} %snap_ref.1), custom_call_target="tpu_custom_call" | custom-call | tf_op jit(solution)/shard_map/pallas_call | solution.py:324
  32.2 3.3 %shard_map.59 = (f32[32,2048]{1,0:T(8,128)}, f32[32,32]{1,0:T(8,128)}, f32[4,32,32]{2,1,0:T(8,128)}) custom-call(f32[32,224]{1,0:T(8,128)} %get-tuple-element.7.coef_ref, f32[32,32]{1,0:T(8,128)} %get-tuple-element.8.energy_ref, f32[4,32,32]{2,1,0:T(8,128)} %get-tuple-element.9.first_ref, bf16[224,2048]{1,0:T(8,128)(2,1)} %get-tuple-element.10.z_ref), custom_call_target="tpu_custom_call" | custom-call | tf_op jit(solution)/shard_map/pallas_call | solution.py:344

commit v4 on v3

--- a/solution.py
+++ b/solution.py
@@ -24,6 +24,10 @@
     return lax.dot_general(
         left, right, (((1,), (1,)), ((), ())), precision=lax.Precision.HIGHEST, preferred_element_type=jnp.float32
     )
+
+
+def narrow(left, right):
+    return jnp.dot(left.astype(jnp.bfloat16), right.astype(jnp.bfloat16), preferred_element_type=jnp.float32)
 
 
 def split(x):
@@ -124,8 +128,10 @@
 
     pl.semaphore_wait(barrier, members - 1 + blocks - 1)
 
-    sends = []
-    for s, (start, stop) in enumerate(STAGES):
+    sends = {}
+
+    def exchange_start(s):
+        start, stop = STAGES[s]
         stage = []
         for step in range(1, ngrp):
             target = lax.rem(grp + step, ngrp)
@@ -136,7 +142,11 @@
             )
             copy.start()
             stage.append(copy)
-        sends.append(stage)
+        sends[s] = stage
+
+    exchange_start(0)
+    exchange_start(1)
+    exchange_start(2)
 
     load_basis.wait()
     base = 3 * rank
@@ -228,18 +238,19 @@
     sub = lax.broadcasted_iota(jnp.int32, (rank, rank), 0)
     eye = sub == lane[:, :rank]
     coef = (lane == lax.broadcasted_iota(jnp.int32, (rank, 4 * rank), 0)).astype(jnp.float32)
+    identity = eye.astype(jnp.float32)
     core = core_ref[...]
     spots = (3, 1, 2)
 
     def update(b, state, cross_raw, own):
-        coef, energy, gram_basis = state
+        coef, energy, excess = state
         diagonal = jnp.where(eye, own, 0.0)
         inverse_col = lax.rsqrt(jnp.sum(diagonal, axis=1, keepdims=True) + epsilon)
         inverse_row = lax.rsqrt(jnp.sum(diagonal, axis=0, keepdims=True) + epsilon)
         cross = mt(coef, cross_raw * inverse_col)
         first_ref[b] = cross
-        total = cross + (cross - mm(gram_basis, cross))
-        w1 = mm(energy, gram_basis) + mt(total, cross)
+        total = cross - narrow(excess, cross)
+        w1 = energy + narrow(energy, excess) + mt(total, cross)
         w2 = mm(energy, cross) + mm(total, own * inverse_col * inverse_row)
         w1_energy = mm(w1, energy)
         square = w1_energy + mt(w2, total)
@@ -249,16 +260,17 @@
             at = spots[b]
             strip = widen(jnp.concatenate([jnp.zeros((rank, at * rank), jnp.float32), placed], axis=1))
             kept = kept + strip
+        bundle = jnp.concatenate([w1, w2, w1_energy, square], axis=1)
         inverse = eliminate(square)
         coef = mm(inverse, kept)
+        bundle = mm(inverse, bundle)
         if b == batches - 1:
             coef = (coef, mm(inverse, placed))
         else:
-            gram_basis = mt(mm(inverse, square), inverse)
-        n1 = mm(inverse, w1)
-        n2 = mm(inverse, w2)
-        energy = mt(mm(inverse, w1_energy), n1) + mt(n2, n2)
-        return coef, energy, gram_basis
+            excess = mt(bundle[:, base:], inverse) - identity
+        n2 = bundle[:, rank:2 * rank]
+        energy = mt(bundle[:, 2 * rank:base], bundle[:, :rank]) + mt(n2, n2)
+        return coef, energy, excess
 
     reduce_start(0)
     reduce_start(1)
@@ -268,7 +280,7 @@
     store_z.start()
     gather_start(1)
     sums, = gather_wait(0)
-    state = (coef, mt(core, core), sums[:, rank:2 * rank])
+    state = (coef, mt(core, core), sums[:, rank:2 * rank] - identity)
     gather_start(2)
     state = update(0, state, sums, sums[:, base:])
     sums, = gather_wait(1)
@@ -296,9 +308,9 @@
     rank = energy_ref.shape[0]
     first_out[...] = first_ref[...]
     pieces = jnp.concatenate([p.astype(jnp.float32) for p in split(coef_ref[...])], axis=0).astype(jnp.bfloat16)
-    core_out[...] = eliminate(energy_ref[...], want_lower=True)
     load.wait()
     wide = jnp.dot(pieces, z[...], preferred_element_type=jnp.float32)
+    core_out[...] = eliminate(energy_ref[...], want_lower=True)
     basis_out[...] = wide[:rank] + wide[rank:2 * rank] + wide[2 * rank:]
 
 

time: 35.8 us -> 35.5 us (level)
    pallas_call x1, Pallas kernels: 31.5 us -> 31.1 us  [body(): pl.pallas_call(functools.partial(fused_kernel, nrows, ngrp), out_shape=(j...]
where the time goes in v4:
time: 35.5 us; the launch traced here: 35.3 us
  Pallas kernels  34.6 us (97%)
  between operations  0.64 us (2%)
    pallas_call x1, Pallas kernels, body(): pl.pallas_call(functools.partial(fused_kernel, nrows, ngrp), out_shape=(j...  31.1 us
    pallas_call x1, Pallas kernels, body(): pl.pallas_call(final_kernel, out_shape=(jax.ShapeDtypeStruct((rank, width...  3.5 us

profile of v4, /device:TPU:0, one launch (start us, length us, event | category | flops | bytes accessed | tf_op | source)
XLA Modules:
  0.0 35.3 jit_solution(12958165364379665749)
XLA Ops:
  0.6 31.1 %shard_map.58 = (bf16[224,2048]{1,0:T(8,128)(2,1)}, f32[32,224]{1,0:T(8,128)}, f32[32,32]{1,0:T(8,128)}, f32[4,32,32]{2,1,0:T(8,128)}) custom-call(f32[32,2048]{1,0:T(8,128)} %basis_ref.1, f32[32,32]{1,0:T(8,128)} %core_ref.1, bf16[4,8,8192]{2,1,0:T(8,128)(2,1)} %snap_ref.1), custom_call_target="tpu_custom_call" | custom-call | tf_op jit(solution)/shard_map/pallas_call | solution.py:336
  31.8 3.5 %shard_map.59 = (f32[32,2048]{1,0:T(8,128)}, f32[32,32]{1,0:T(8,128)}, f32[4,32,32]{2,1,0:T(8,128)}) custom-call(f32[32,224]{1,0:T(8,128)} %get-tuple-element.7.coef_ref, f32[32,32]{1,0:T(8,128)} %get-tuple-element.8.energy_ref, f32[4,32,32]{2,1,0:T(8,128)} %get-tuple-element.9.first_ref, bf16[224,2048]{1,0:T(8,128)(2,1)} %get-tuple-element.10.z_ref), custom_call_target="tpu_custom_call" | custom-call | tf_op jit(solution)/shard_map/pallas_call | solution.py:356
